TPU v7x, 32 devices: a whole 2x2x4 slice. The times are simulated.
32 devices in a mesh: expert: 8 (over y, x, core), dp: 4 (over z).
Axes of the slice: x: 2, y: 2, z: 4, core: 2. Of those that a mesh axis runs over, the one named last changes fastest.
Arguments:
- gradient: bfloat16 [4, 1, 14336, 2048], P('dp', None, None, 'expert'), may hold values from -6 to 6
- momentum: float32 [4, 1, 14336, 2048], P('dp', None, 'expert'), may hold values from -6 to 6
- group_index: int32 [224, 32, 4, 32], P('expert'), may hold values from 0 to 4095, all different within a row
Outputs:
- momentum_next: float32 [4, 1, 14336, 2048], P('dp', None, 'expert')
- update: float32 [1, 14336, 2048], P(None, None, 'expert')
Inputs may be any that keep to these rules, and one draw needn't show every extreme that they name: `group_index`: an entry names the coefficient at row frequency (entry // 64) and column frequency (entry % 64) of its block; the 32 entries of one block and replica differ.
All inputs are finite; a program needn't handle non-finite values.
Results may differ from a plain program's by a relative error of at most 0.0003.
Values may be sent and summed in bfloat16 or wider, within the bound.
No kernel may reach another device: no remote copies, remote signals or barrier semaphores. Data moves between devices by JAX's collectives and lax.ppermute only.
A program may use at most 192 MiB of HBM per device.

v0:
```python
import math
import jax
import jax.numpy as jnp
from jax import lax
from jax.sharding import PartitionSpec as P

SPAN = 64
MOMENTUM_DECAY = 0.999
HIGHEST_PRECISION = lax.Precision.HIGHEST


def cosine_table(order_size):
    frequency = jnp.arange(order_size, dtype=jnp.float32)[:, None]
    position = jnp.arange(order_size, dtype=jnp.float32)[None, :]
    weighting = jnp.where(frequency == 0, math.sqrt(1.0 / order_size), math.sqrt(2.0 / order_size))
    return weighting * jnp.cos(math.pi * (2.0 * position + 1.0) * frequency / (2.0 * order_size))


def forward(blocks, cosine):
    return jnp.einsum("ui,piqj,vj->pquv", cosine, blocks, cosine, precision=HIGHEST_PRECISION)


def inverse(coeffs, cosine):
    return jnp.einsum("ui,pquv,vj->piqj", cosine, coeffs, cosine, precision=HIGHEST_PRECISION)


def place(values, picked, total):
    count_rows = picked.shape[0]
    count_cols = picked.shape[1]
    row_ids = jnp.arange(count_rows, dtype=jnp.int32)[:, None, None]
    col_ids = jnp.arange(count_cols, dtype=jnp.int32)[None, :, None]
    empty = jnp.zeros((count_rows, count_cols, total), jnp.float32)
    return empty.at[row_ids, col_ids, picked].add(values)


def on_device(gradient, momentum, group_index):
    cosine = cosine_table(SPAN)
    replica = lax.axis_index("dp")
    shifted = lax.all_to_all(gradient, "expert", split_axis=2, concat_axis=3, tiled=True)
    row_count = shifted.shape[1] * shifted.shape[2]
    col_count = shifted.shape[3]
    decayed = MOMENTUM_DECAY * momentum.reshape(row_count, col_count) + shifted.reshape(
        row_count, col_count
    ).astype(jnp.float32)
    block_rows = row_count // SPAN
    block_cols = col_count // SPAN
    blocks = decayed.reshape(block_rows, SPAN, block_cols, SPAN)
    coeffs = forward(blocks, cosine).reshape(block_rows, block_cols, SPAN * SPAN)
    own = lax.dynamic_index_in_dim(group_index, replica, 2, keepdims=False)
    values = jnp.take_along_axis(coeffs, own, axis=2)
    selected = place(values, own, SPAN * SPAN).reshape(block_rows, block_cols, SPAN, SPAN)
    restored = inverse(selected, cosine).reshape(row_count, col_count)
    momentum_next = (decayed - restored).reshape(momentum.shape)
    total = lax.psum(restored, "dp")
    update = lax.all_to_all(total[None], "expert", split_axis=2, concat_axis=1, tiled=True)
    return (momentum_next, update)


def solution(mesh):
    placed = (
        P("dp", None, None, "expert"),
        P("dp", None, "expert", None),
        P("expert", None, None, None),
    )
    return jax.shard_map(
        on_device,
        mesh=mesh,
        in_specs=placed,
        out_specs=(P("dp", None, "expert", None), P(None, None, "expert")),
        check_vma=False,
    )
```

profile of v0, /device:TPU:0, one launch (start us, length us, event | category | flops | bytes accessed | tf_op | source)
XLA Modules:
  0.0 1791.6 jit_solution(7726705985942069426)
XLA Ops:
  7.2 13.9 copy.47
  21.6 74.4 %reduce.4 = bf16[14336,256]{1,0:T(8,128)(2,1)} reduce(bf16[14336,1,1,256]{3,2,1,0:T(2,128)(2,1)} %bitcast.50, bf16[]{:T(256)} %broadcast.103), dimensions={1,2}, to_apply=%bitcast.46.reduce_sub_computation | reduce | bytes 14680066
  96.0 9.0 reshape.130
  105.1 5.2 all-to-all-start
  111.4 0.8 copy-done.2
  113.1 0.8 reshape.121
  113.9 14.1 broadcast_multiply_fusion
  128.0 24.3 %mul.98 = f32[28,64,32,64]{3,2,1,0:T(8,128)} reshape(f32[1,1,1792,2048]{3,2,1,0:T(8,128)} %broadcast_multiply_fusion) | data formatting | bytes 29360128 | tf_op jit(solution)/shard_map/mul | solution.py:42
  152.5 40.9 %all-to-all-done = bf16[8,2,229376]{2,1,0:T(2,128)(2,1)} async-done(((bf16[8,2,229376]{2,1,0:T(2,128)(2,1)}), bf16[8,2,229376]{2,1,0:T(2,128)(2,1)}, u32[]{:S(2)}, u32[]{:S(2)}) %all-to-all-start) | async-done | bytes 7340064 | tf_op jit(solution)/shard_map/all_to_all | solution.py:39
  193.4 12.1 reshape.131
  205.5 15.9 copy.46
  221.4 21.6 %reshape.112 = f32[28,64,32,64]{3,2,1,0:T(8,128)} reshape(f32[1,1,1792,8,256]{4,3,2,1,0:T(8,128)} %bitcast.47) | data formatting | bytes 29360128 | tf_op jit(solution)/shard_map/convert_element_type | solution.py:44
  243.1 29.9 %add.64 = f32[28,64,32,64]{3,2,1,0:T(8,128)} add(f32[28,64,32,64]{3,2,1,0:T(8,128)} %mul.98, f32[28,64,32,64]{3,2,1,0:T(8,128)} %reshape.112) | non-fusion elementwise | flops 3670016 | bytes 44040192 | tf_op jit(solution)/shard_map/add | solution.py:42
  273.0 52.6 %fusion = f32[28,32,64,64]{2,3,1,0:T(8,128)} fusion(f32[28,64,32,64]{3,2,1,0:T(8,128)} %add.64, f32[64]{0:T(128)S(1)} %get-tuple-element.5, f32[64]{0:T(128)S(1)} %get-tuple-element.4), kind=kOutput, calls=%fused_computation.2 | convolution fusion | flops 2818584576 | bytes 29360640 | tf_op jit(solution)/shard_map/ui,piqj,vj->pquv/dot_general | solution.py:20
  325.6 29.6 %fusion.7 = f32[28,32,64,64]{3,2,1,0:T(8,128)} fusion(f32[28,32,64,64]{2,3,1,0:T(8,128)} %fusion, f32[64]{0:T(128)S(1)} %get-tuple-element.5, f32[64]{0:T(128)S(1)} %get-tuple-element.4), kind=kOutput, calls=%fused_computation.21 | convolution fusion | flops 2818584576 | bytes 29360640 | tf_op jit(solution)/shard_map/ui,piqj,vj->pquv/dot_general | solution.py:20
  355.3 24.7 %reshape.101 = f32[28,32,4096]{2,1,0:T(8,128)} reshape(f32[28,32,64,64]{3,2,1,0:T(8,128)} %fusion.7) | data formatting | bytes 29360128 | tf_op jit(solution)/shard_map/reshape | solution.py:48
  380.0 398.1 %gather_fusion = f32[28672]{0:T(1024)S(1)} fusion(f32[28,32,4096]{2,1,0:T(8,128)} %reshape.101, s32[28672]{0:T(1024)S(1)} %reshape.115), kind=kCustom, calls=%fused_computation | custom fusion | bytes 573440 | tf_op jit(solution)/shard_map/jit(take_along_axis)/gather | solution.py:50
  778.6 156.3 %scatter_custom_fusion = f32[3670016]{0:T(1024)} fusion(s32[28672]{0:T(1024)} %reshape.121, f32[28672]{0:T(1024)S(1)} %reshape.123, f32[]{:T(128)} %constant.15.clone.1), kind=kCustom, calls=%fused_computation.7 | custom fusion | flops 28672 | bytes 14680576
  934.9 22.2 %reshape.102 = f32[28,32,64,64]{3,2,1,0:T(8,128)} reshape(f32[3670016]{0:T(1024)} %scatter_custom_fusion) | data formatting | bytes 29360128 | tf_op jit(solution)/shard_map/reshape | solution.py:51
  957.1 34.3 %fusion.5 = f32[28,32,64,64]{2,3,1,0:T(8,128)} fusion(f32[28,32,64,64]{3,2,1,0:T(8,128)} %reshape.102, f32[64]{0:T(128)S(1)} %copy-done.7, f32[64]{0:T(128)S(1)} %copy-done.5), kind=kOutput, calls=%fused_computation.19 | convolution fusion | flops 2818584576 | bytes 29360640 | tf_op jit(solution)/shard_map/ui,pquv,vj->piqj/dot_general | solution.py:24
  991.3 29.2 %convolution_bitcast_fusion = f32[28,64,32,64]{3,1,2,0:T(8,128)S(1)} fusion(f32[28,32,64,64]{2,3,1,0:T(8,128)} %fusion.5, f32[64]{0:T(128)S(1)} %copy-done.7, f32[64]{0:T(128)S(1)} %copy-done.5), kind=kOutput, calls=%fused_computation.6 | convolution fusion | flops 2818584576 | bytes 29360640 | tf_op jit(solution)/shard_map/ui,pquv,vj->piqj/dot_general | solution.py:24
  1020.6 19.3 %copy.33 = f32[28,64,32,64]{3,2,1,0:T(8,128)} copy(f32[28,64,32,64]{3,1,2,0:T(8,128)S(1)} %convolution_bitcast_fusion) | data formatting | bytes 29360128 | tf_op jit(solution)/shard_map/ui,pquv,vj->piqj/transpose | solution.py:24
  1039.9 25.4 %broadcast_in_dim.39 = f32[1,1792,2048]{2,1,0:T(8,128)} reshape(f32[28,64,32,64]{3,2,1,0:T(8,128)} %copy.33) | data formatting | bytes 29360128 | tf_op jit(solution)/shard_map/broadcast_in_dim | solution.py:55
  1065.3 494.5 %all-reduce.2.cloned.1.call-done = f32[1,1792,2048]{2,1,0:T(8,128)} async-done(((f32[1,1792,2048]{2,1,0:T(8,128)}), f32[1,1792,2048]{2,1,0:T(8,128)}) %all-reduce.2.cloned.1.call-update) | async-done | bytes 14680080 | tf_op jit(solution)/shard_map/psum | solution.py:54
  1559.7 32.1 %copy.35 = f32[1,1792,2048]{1,0,2:T(1,128)} copy(f32[1,1792,2048]{2,1,0:T(8,128)} %all-reduce.2.cloned.1.call-done) | data formatting | bytes 29360128 | tf_op jit(solution)/shard_map/psum | solution.py:54
  1591.8 5.6 all-to-all-start.1
  1597.4 25.4 %reshape.103 = f32[1,1,1792,2048]{3,2,1,0:T(8,128)} reshape(f32[28,64,32,64]{3,2,1,0:T(8,128)} %copy.33) | data formatting | bytes 29360128 | tf_op jit(solution)/shard_map/reshape | solution.py:52
  1622.8 15.8 reshape.111
  1638.6 20.9 %add_subtract_fusion = f32[1,1,1792,2048]{3,2,1,0:T(8,128)} fusion(f32[1,1,1792,2048]{3,2,1,0:T(8,128)} %reshape.103, f32[1,1,1792,2048]{3,2,1,0:T(8,128)} %reshape.111, f32[1,1,1792,2048]{3,2,1,0:T(8,128)} %param.4), kind=kLoop, calls=%fused_computation.5 | loop fusion | flops 11010048 | bytes 58720256 | tf_op jit(solution)/shard_map/sub | solution.py:53
  1659.6 99.3 %all-to-all-done.1 = f32[1,1792,2048]{1,0,2:T(1,128)} async-done(((f32[1,1792,2048]{1,0,2:T(1,128)}), f32[1,1792,2048]{1,0,2:T(1,128)}, u32[]{:S(2)}, u32[]{:S(2)}) %all-to-all-start.1) | async-done | bytes 14680096 | tf_op jit(solution)/shard_map/all_to_all | solution.py:55
  1758.9 11.3 copy.41
  1770.2 14.4 copy.36
  (34 shorter events, 3.1 us)
Async XLA Ops:
  7.2 103.7 %copy-start = (s32[28,32,4,32]{3,2,1,0:T(4,128)S(1)}, s32[28,32,4,32]{3,2,1,0:T(4,128)}, u32[]{:S(2)}) copy-start(s32[28,32,4,32]{3,2,1,0:T(4,128)} %param.5) | copy-start | bytes 1376260
  96.0 16.4 copy-start.9
  96.0 16.6 copy-start.8
  105.1 88.4 %all-to-all-start = ((bf16[8,2,229376]{2,1,0:T(2,128)(2,1)}), bf16[8,2,229376]{2,1,0:T(2,128)(2,1)}, u32[]{:S(2)}, u32[]{:S(2)}) async-start(bf16[8,2,229376]{2,1,0:T(2,128)(2,1)} %reshape.130), calls=%async_computation | async-start | bytes 14680064 | tf_op jit(solution)/shard_map/all_to_all | solution.py:39
  110.3 1449.5 %all-reduce.2.cloned.1.call-start = ((), (), s32[]{:S(2)}) async-start(), calls=%async_computation.2 | async-start | bytes 29360128 | tf_op jit(solution)/shard_map/psum | solution.py:54
  111.3 0.8 copy-start.2
  152.5 173.1 %copy-start.4 = (f32[64]{0:T(128)}, f32[64]{0:T(128)S(1)}, u32[]{:S(2)}) copy-start(f32[64]{0:T(128)S(1)} %get-tuple-element.4) | copy-start | bytes 772
  152.5 173.1 %copy-start.6 = (f32[64]{0:T(128)}, f32[64]{0:T(128)S(1)}, u32[]{:S(2)}) copy-start(f32[64]{0:T(128)S(1)} %get-tuple-element.5) | copy-start | bytes 772
  380.0 398.3 %copy-start.3 = (s32[28,32,1,32]{3,2,1,0:T(1,128)S(1)}, s32[28,32,1,32]{3,2,1,0:T(1,128)}, u32[]{:S(2)}) copy-start(s32[28,32,1,32]{3,2,1,0:T(1,128)} %copy-done.2) | copy-start | bytes 344068
  934.9 22.2 %copy-start.5 = (f32[64]{0:T(128)S(1)}, f32[64]{0:T(128)}, u32[]{:S(2)}) copy-start(f32[64]{0:T(128)} %copy-done.4) | copy-start | bytes 772
  934.9 22.2 %copy-start.7 = (f32[64]{0:T(128)S(1)}, f32[64]{0:T(128)}, u32[]{:S(2)}) copy-start(f32[64]{0:T(128)} %copy-done.6) | copy-start | bytes 772
  1591.8 167.0 %all-to-all-start.1 = ((f32[1,1792,2048]{1,0,2:T(1,128)}), f32[1,1792,2048]{1,0,2:T(1,128)}, u32[]{:S(2)}, u32[]{:S(2)}) async-start(f32[1,1792,2048]{1,0,2:T(1,128)} %copy.35), calls=%async_computation.1 | async-start | bytes 29360128 | tf_op jit(solution)/shard_map/all_to_all | solution.py:55
  1770.2 14.4 copy-start.1
Sparse Core Ops, SparseCore 0:
  1065.4 494.3 all-reduce.1
where the time goes:
time: 1810 us; the launch traced here: 1790 us
  local copies, waits for them, and re-layouts  689 us (38%)
  waiting for transfers between devices  635 us (35%)
  other arithmetic  297 us (16%)
  matrix products  146 us (8%)
    psum x1, waiting for transfers between devices, on_device(): total = lax.psum(restored, 'dp')  494 us
    gather x2, local copies, waits for them, and re-layouts, on_device(): values = jnp.take_along_axis(coeffs, own, axis=2)  398 us
    unnamed x5, other arithmetic  231 us
    all_to_all x1, waiting for transfers between devices, on_device(): lax.all_to_all(total[None], 'expert', split_axis=2, concat_axis=1, tiled=...  99.3 us
    dot_general x2, matrix products, forward(): jnp.einsum('ui,piqj,vj->pquv', cosine, blocks, cosine, precision=HIGHEST_...  82.3 us
    dot_general x2, matrix products, inverse(): jnp.einsum('ui,pquv,vj->piqj', cosine, coeffs, cosine, precision=HIGHEST_...  63.5 us
    convert_element_type x3, local copies, waits for them, and re-layouts, on_device(): decayed = MOMENTUM_DECAY * momentum.reshape(row_count, col_count) + shift...  53.4 us
    unnamed x26, local copies, waits for them, and re-layouts  48.5 us
  transfers between devices with their start and end apart: 3, of which 3 were waited for; matrix products, arithmetic and copies ran while one was open for 6% of the time, Pallas kernels for 0%

commit v1 on v0

--- a/solution.py
+++ b/solution.py
@@ -51,7 +51,9 @@
     selected = place(values, own, SPAN * SPAN).reshape(block_rows, block_cols, SPAN, SPAN)
     restored = inverse(selected, cosine).reshape(row_count, col_count)
     momentum_next = (decayed - restored).reshape(momentum.shape)
-    total = lax.psum(restored, "dp")
+    total = restored
+    for hop in (1, 2):
+        total = total + lax.ppermute(total, "dp", [(dev, dev ^ hop) for dev in range(4)])
     update = lax.all_to_all(total[None], "expert", split_axis=2, concat_axis=1, tiled=True)
     return (momentum_next, update)
 

time: 1810 us -> 2270 us (1.25)
  waiting for transfers between devices: 635 us -> 1080 us
    ppermute x0 -> x2, waiting for transfers between devices: none -> 939 us  [on_device(): lax.ppermute(total, 'dp', [(dev, dev ^ hop) for dev in range(4)])]
    psum x1 -> x0, waiting for transfers between devices: 494 us -> none  [on_device(): total = lax.psum(restored, 'dp')]
    psum x1 -> x0, local copies, waits for them, and re-layouts: 32.1 us -> none  [on_device(): total = lax.psum(restored, 'dp')]
    reshape x1 -> x2, local copies, waits for them, and re-layouts: 25.4 us -> 50.8 us  [on_device(): restored = inverse(selected, cosine).reshape(row_count, col_count)]
  transfers between devices with their start and end apart: 3 -> 4, of which waited for: 3 -> 4; matrix products, arithmetic and copies ran while one was open for 6% -> 5% of each run, Pallas kernels for 0% -> 0%
where the time goes in v1:
time: 2270 us; the launch traced here: 2250 us
  waiting for transfers between devices  1080 us (48%)
  local copies, waits for them, and re-layouts  689 us (30%)
  other arithmetic  310 us (14%)
  matrix products  146 us (6%)
    ppermute x2, waiting for transfers between devices, on_device(): lax.ppermute(total, 'dp', [(dev, dev ^ hop) for dev in range(4)])  939 us
    gather x2, local copies, waits for them, and re-layouts, on_device(): values = jnp.take_along_axis(coeffs, own, axis=2)  398 us
    unnamed x5, other arithmetic  232 us
    all_to_all x1, waiting for transfers between devices, on_device(): lax.all_to_all(total[None], 'expert', split_axis=2, concat_axis=1, tiled=...  99.5 us
    dot_general x2, matrix products, forward(): jnp.einsum('ui,piqj,vj->pquv', cosine, blocks, cosine, precision=HIGHEST_...  82.3 us
    dot_general x2, matrix products, inverse(): jnp.einsum('ui,pquv,vj->piqj', cosine, coeffs, cosine, precision=HIGHEST_...  63.5 us
    convert_element_type x3, local copies, waits for them, and re-layouts, on_device(): decayed = MOMENTUM_DECAY * momentum.reshape(row_count, col_count) + shift...  53.4 us
    reshape x2, local copies, waits for them, and re-layouts, on_device(): restored = inverse(selected, cosine).reshape(row_count, col_count)  50.8 us
  transfers between devices with their start and end apart: 4, of which 4 were waited for; matrix products, arithmetic and copies ran while one was open for 5% of the time, Pallas kernels for 0%

profile of v1, /device:TPU:0, one launch (start us, length us, event | category | flops | bytes accessed | tf_op | source)
XLA Modules:
  0.0 2245.1 jit_solution(3388913348840540729)
XLA Ops:
  0.6 13.9 copy.47
  15.1 74.5 %reduce.4 = bf16[14336,256]{1,0:T(8,128)(2,1)} reduce(bf16[14336,1,1,256]{3,2,1,0:T(2,128)(2,1)} %bitcast.52, bf16[]{:T(256)} %broadcast.103), dimensions={1,2}, to_apply=%bitcast.48.reduce_sub_computation | reduce | bytes 14680066
  89.6 9.0 reshape.129
  107.6 14.1 broadcast_multiply_fusion
  121.6 24.3 %mul.98 = f32[28,64,32,64]{3,2,1,0:T(8,128)} reshape(f32[1,1,1792,2048]{3,2,1,0:T(8,128)} %broadcast_multiply_fusion) | data formatting | bytes 29360128 | tf_op jit(solution)/shard_map/mul | solution.py:42
  146.2 41.4 %all-to-all-done = bf16[8,2,229376]{2,1,0:T(2,128)(2,1)} async-done(((bf16[8,2,229376]{2,1,0:T(2,128)(2,1)}), bf16[8,2,229376]{2,1,0:T(2,128)(2,1)}, u32[]{:S(2)}, u32[]{:S(2)}) %all-to-all-start) | async-done | bytes 7340064 | tf_op jit(solution)/shard_map/all_to_all | solution.py:39
  187.5 12.1 reshape.130
  199.7 15.9 copy.46
  215.6 21.7 reshape.111
  237.2 29.9 %add.68 = f32[28,64,32,64]{3,2,1,0:T(8,128)} add(f32[28,64,32,64]{3,2,1,0:T(8,128)} %mul.98, f32[28,64,32,64]{3,2,1,0:T(8,128)} %reshape.111) | non-fusion elementwise | flops 3670016 | bytes 44040192 | tf_op jit(solution)/shard_map/add | solution.py:42
  267.1 52.7 %fusion = f32[28,32,64,64]{2,3,1,0:T(8,128)} fusion(f32[28,64,32,64]{3,2,1,0:T(8,128)} %add.68, f32[64]{0:T(128)S(1)} %get-tuple-element.5, f32[64]{0:T(128)S(1)} %get-tuple-element.4), kind=kOutput, calls=%fused_computation.2 | convolution fusion | flops 2818584576 | bytes 29360640 | tf_op jit(solution)/shard_map/ui,piqj,vj->pquv/dot_general | solution.py:20
  319.8 29.7 %fusion.7 = f32[28,32,64,64]{3,2,1,0:T(8,128)} fusion(f32[28,32,64,64]{2,3,1,0:T(8,128)} %fusion, f32[64]{0:T(128)S(1)} %get-tuple-element.5, f32[64]{0:T(128)S(1)} %get-tuple-element.4), kind=kOutput, calls=%fused_computation.22 | convolution fusion | flops 2818584576 | bytes 29360640 | tf_op jit(solution)/shard_map/ui,piqj,vj->pquv/dot_general | solution.py:20
  349.5 24.7 %reshape.101 = f32[28,32,4096]{2,1,0:T(8,128)} reshape(f32[28,32,64,64]{3,2,1,0:T(8,128)} %fusion.7) | data formatting | bytes 29360128 | tf_op jit(solution)/shard_map/reshape | solution.py:48
  374.2 398.1 %gather_fusion = f32[28672]{0:T(1024)S(1)} fusion(f32[28,32,4096]{2,1,0:T(8,128)} %reshape.101, s32[28672]{0:T(1024)S(1)} %reshape.114), kind=kCustom, calls=%fused_computation | custom fusion | bytes 573440 | tf_op jit(solution)/shard_map/jit(take_along_axis)/gather | solution.py:50
  772.8 156.3 %scatter_custom_fusion = f32[3670016]{0:T(1024)} fusion(s32[28672]{0:T(1024)} %reshape.120, f32[28672]{0:T(1024)S(1)} %reshape.122, f32[]{:T(128)} %constant.15.clone.1), kind=kCustom, calls=%fused_computation.8 | custom fusion | flops 28672 | bytes 14680576
  929.1 22.2 reshape.102
  951.3 34.3 %fusion.5 = f32[28,32,64,64]{2,3,1,0:T(8,128)} fusion(f32[28,32,64,64]{3,2,1,0:T(8,128)} %reshape.102, f32[64]{0:T(128)S(1)} %copy-done.7, f32[64]{0:T(128)S(1)} %copy-done.5), kind=kOutput, calls=%fused_computation.20 | convolution fusion | flops 2818584576 | bytes 29360640 | tf_op jit(solution)/shard_map/ui,pquv,vj->piqj/dot_general | solution.py:24
  985.6 29.2 %convolution_bitcast_fusion = f32[28,64,32,64]{3,1,2,0:T(8,128)S(1)} fusion(f32[28,32,64,64]{2,3,1,0:T(8,128)} %fusion.5, f32[64]{0:T(128)S(1)} %copy-done.7, f32[64]{0:T(128)S(1)} %copy-done.5), kind=kOutput, calls=%fused_computation.7 | convolution fusion | flops 2818584576 | bytes 29360640 | tf_op jit(solution)/shard_map/ui,pquv,vj->piqj/dot_general | solution.py:24
  1014.8 19.3 copy.33
  1034.1 25.4 %reshape.104 = f32[1792,2048]{1,0:T(8,128)} reshape(f32[28,64,32,64]{3,2,1,0:T(8,128)} %copy.33) | data formatting | bytes 29360128 | tf_op jit(solution)/shard_map/reshape | solution.py:52
  1062.2 312.7 %collective-permute-done = f32[1792,2048]{1,0:T(8,128)S(1)} collective-permute-done((f32[1792,2048]{1,0:T(8,128)}, f32[1792,2048]{1,0:T(8,128)S(1)}, u32[]{:S(2)}, u32[]{:S(2)}) %collective-permute-start) | collective-permute-done | bytes 14680096 | tf_op jit(solution)/shard_map/ppermute | solution.py:56
  1374.9 6.9 add.71
  1384.8 626.6 %collective-permute-done.1 = f32[1792,2048]{1,0:T(8,128)S(1)} collective-permute-done((f32[1792,2048]{1,0:T(8,128)S(1)}, f32[1792,2048]{1,0:T(8,128)S(1)}, u32[]{:S(2)}, u32[]{:S(2)}) %collective-permute-start.1) | collective-permute-done | bytes 14680096 | tf_op jit(solution)/shard_map/ppermute | solution.py:56
  2011.5 6.4 add_bitcast_fusion
  2017.9 32.0 %copy.35 = f32[1,1792,2048]{1,0,2:T(1,128)} copy(f32[1,1792,2048]{2,1,0:T(8,128)} %add_bitcast_fusion) | data formatting | bytes 29360128 | tf_op jit(solution)/shard_map/broadcast_in_dim | solution.py:57
  2049.9 7.6 all-to-all-start.1
  2057.5 25.4 %reshape.103 = f32[1,1,1792,2048]{3,2,1,0:T(8,128)} reshape(f32[28,64,32,64]{3,2,1,0:T(8,128)} %copy.33) | data formatting | bytes 29360128 | tf_op jit(solution)/shard_map/reshape | solution.py:52
  2082.9 15.8 reshape.110
  2098.7 20.9 add_subtract_fusion
  2119.7 99.5 %all-to-all-done.1 = f32[1,1792,2048]{1,0,2:T(1,128)} async-done(((f32[1,1792,2048]{1,0,2:T(1,128)}), f32[1,1792,2048]{1,0,2:T(1,128)}, u32[]{:S(2)}, u32[]{:S(2)}) %all-to-all-start.1) | async-done | bytes 14680096 | tf_op jit(solution)/shard_map/all_to_all | solution.py:57
  2219.2 11.3 copy.41
  2230.5 14.4 copy.36
  (37 shorter events, 15.6 us)
Async XLA Ops:
  0.6 103.8 %copy-start = (s32[28,32,4,32]{3,2,1,0:T(4,128)S(1)}, s32[28,32,4,32]{3,2,1,0:T(4,128)}, u32[]{:S(2)}) copy-start(s32[28,32,4,32]{3,2,1,0:T(4,128)} %param.5) | copy-start | bytes 1376260
  89.6 16.4 copy-start.9
  89.6 16.7 copy-start.8
  98.7 88.9 %all-to-all-start = ((bf16[8,2,229376]{2,1,0:T(2,128)(2,1)}), bf16[8,2,229376]{2,1,0:T(2,128)(2,1)}, u32[]{:S(2)}, u32[]{:S(2)}) async-start(bf16[8,2,229376]{2,1,0:T(2,128)(2,1)} %reshape.129), calls=%async_computation | async-start | bytes 14680064 | tf_op jit(solution)/shard_map/all_to_all | solution.py:39
  105.0 0.8 copy-start.2
  146.1 173.7 %copy-start.4 = (f32[64]{0:T(128)}, f32[64]{0:T(128)S(1)}, u32[]{:S(2)}) copy-start(f32[64]{0:T(128)S(1)} %get-tuple-element.4) | copy-start | bytes 772
  146.1 173.7 %copy-start.6 = (f32[64]{0:T(128)}, f32[64]{0:T(128)S(1)}, u32[]{:S(2)}) copy-start(f32[64]{0:T(128)S(1)} %get-tuple-element.5) | copy-start | bytes 772
  374.2 398.3 %copy-start.3 = (s32[28,32,1,32]{3,2,1,0:T(1,128)S(1)}, s32[28,32,1,32]{3,2,1,0:T(1,128)}, u32[]{:S(2)}) copy-start(s32[28,32,1,32]{3,2,1,0:T(1,128)} %copy-done.2) | copy-start | bytes 344068
  929.1 22.2 copy-start.5
  929.1 22.2 copy-start.7
  1059.5 315.4 %collective-permute-start = (f32[1792,2048]{1,0:T(8,128)}, f32[1792,2048]{1,0:T(8,128)S(1)}, u32[]{:S(2)}, u32[]{:S(2)}) collective-permute-start(f32[1792,2048]{1,0:T(8,128)} %reshape.104), channel_id=1, source_target_pairs={{0,1},{1,0},{2,3},{3,2},{4,5},{5,4},{6,7},{7,6},{8,9},{9,8},{10,11... | collective-permute-start | bytes 44040200 | tf_op jit(solution)/shard_map/ppermute | solution.py:56
  1381.9 629.6 %collective-permute-start.1 = (f32[1792,2048]{1,0:T(8,128)S(1)}, f32[1792,2048]{1,0:T(8,128)S(1)}, u32[]{:S(2)}, u32[]{:S(2)}) collective-permute-start(f32[1792,2048]{1,0:T(8,128)S(1)} %add.71), channel_id=1, source_target_pairs={{0,2},{1,3},{2,0},{3,1},{4,6},{5,7},{6,4},{7,5},{8,10},{9,11},{10,... | collective-permute-start | bytes 44040200 | tf_op jit(solution)/shard_map/ppermute | solution.py:56
  2049.9 169.3 %all-to-all-start.1 = ((f32[1,1792,2048]{1,0,2:T(1,128)}), f32[1,1792,2048]{1,0,2:T(1,128)}, u32[]{:S(2)}, u32[]{:S(2)}) async-start(f32[1,1792,2048]{1,0,2:T(1,128)} %copy.35), calls=%async_computation.1 | async-start | bytes 29360128 | tf_op jit(solution)/shard_map/all_to_all | solution.py:57
  2230.5 14.4 copy-start.1
